TPU v7x, 32 devices: a whole 2x2x4 slice. The times are simulated.
32 devices in a mesh: row: 4 (over y, x), col: 4 (over z), depth: 2 (over core).
Axes of the slice: x: 2, y: 2, z: 4, core: 2. Of those that a mesh axis runs over, the one named last changes fastest.
Arguments:
- matrix_columns: float32 [4, 8, 768, 24576], P(None, ('col', 'depth'), None, 'row'), may hold values from -0.0390625 to 0.0390625
- sources: float32 [4, 8, 768, 128], P('row', ('col', 'depth')), may hold values from -6 to 6
Outputs:
- first_image: float32 [4, 8, 768, 128], P('row', ('col', 'depth'))
- second_image: float32 [4, 8, 768, 128], P('row', ('col', 'depth'))
All inputs are finite; a program needn't handle non-finite values.
Results may differ from a plain program's by a relative error of at most 0.00011.
Values sent between devices are 32-bit elements; how exact they have to be, the bound alone decides.
A program may use at most 128 MiB of HBM per device.

v0:
```python
import functools

import jax
import jax.numpy as jnp
from jax import lax
from jax.experimental import pallas as pl
from jax.experimental.pallas import tpu as pltpu
from jax.sharding import PartitionSpec as P

LANES = 256


def split(values):
    high = values.astype(jnp.bfloat16)
    low = (values - high.astype(jnp.float32)).astype(jnp.bfloat16)
    return high, low


def product_kernel(x_ref, a_ref, out_ref, xt_ref):
    width = x_ref.shape[1]
    depth = x_ref.shape[0]
    tile = a_ref.shape[3]

    @pl.when(pl.program_id(0) == 0)
    def _():
        high, low = split(x_ref[...].T)
        xt_ref[:width, :] = high
        xt_ref[width:, :] = low

    for start in range(0, tile, LANES):
        block = a_ref[:, 0, :, start:start + LANES].reshape(depth, LANES)
        high, low = split(block)
        main = jnp.dot(xt_ref[...], high, preferred_element_type=jnp.float32)
        rest = jnp.dot(xt_ref[:width, :], low, preferred_element_type=jnp.float32)
        total = main[:width] + (main[width:] + rest)
        out_ref[start:start + LANES, :] = total.T


def product(columns, inputs_flat):
    outer, _, piece, rows = columns.shape
    depth, width = inputs_flat.shape
    tile = 2 * LANES
    return pl.pallas_call(
        product_kernel,
        grid=(rows // tile,),
        out_shape=jax.ShapeDtypeStruct((rows, width), jnp.float32),
        in_specs=[
            pl.BlockSpec((depth, width), lambda i: (0, 0)),
            pl.BlockSpec((outer, 1, piece, tile), lambda i: (0, 0, 0, i)),
        ],
        out_specs=pl.BlockSpec((tile, width), lambda i: (i, 0)),
        scratch_shapes=[pltpu.VMEM((2 * width, depth), jnp.bfloat16)],
        compiler_params=pltpu.CompilerParams(
            dimension_semantics=("arbitrary",), vmem_limit_bytes=48 << 20
        ),
        cost_estimate=pl.CostEstimate(
            flops=6 * rows * depth * width, bytes_accessed=4 * rows * depth, transcendentals=0
        ),
    )(inputs_flat, columns)


def apply_once(columns, vector_part):
    piece_len = vector_part.shape[2]
    width = vector_part.shape[3]
    gathered = lax.all_gather(vector_part, "row", axis=0, tiled=True)
    inputs_flat = gathered.reshape(-1, width)
    owned = lax.psum_scatter(
        product(columns, inputs_flat), ("col", "depth"), scatter_dimension=0, tiled=True
    )
    return owned.reshape(1, 1, piece_len, width)


def body(matrix_columns, sources):
    first_image = apply_once(matrix_columns, sources)
    second_image = apply_once(matrix_columns, first_image)
    return (first_image, second_image)


def solution(mesh):
    in_specs = (P(None, ("col", "depth"), None, "row"), P("row", ("col", "depth"), None, None))
    out_specs = (P("row", ("col", "depth"), None, None), P("row", ("col", "depth"), None, None))
    return jax.shard_map(body, mesh=mesh, in_specs=in_specs, out_specs=out_specs, check_vma=False)
```

profile of v0, /device:TPU:0, one launch (start us, length us, event | category | flops | bytes accessed | tf_op | source)
XLA Modules:
  0.0 228.9 jit_solution(8209069307372079450)
XLA Ops:
  7.2 0.0 all-gather.4.cloned.1.call-start
  7.2 0.7 all-gather.4.cloned.1.call-update
  7.9 0.0 reduce-scatter.3.cloned.1.call-start
  7.9 35.5 %all-gather.4.cloned.1.call-done = f32[4,1,768,128]{3,2,1,0:T(8,128)} async-done(((f32[1,1,768,128]{3,2,1,0:T(8,128)}), f32[4,1,768,128]{3,2,1,0:T(8,128)}) %all-gather.4.cloned.1.call-update) | async-done | bytes 1572880 | tf_op jit(solution)/shard_map/all_gather | solution.py:65
  43.4 0.0 copy-start
  43.4 1.4 copy-done
  44.8 31.3 %shard_map.41 = f32[6144,128]{1,0:T(8,128)} custom-call(f32[3072,128]{1,0:T(8,128)S(1)} %bitcast.3, f32[4,1,768,6144]{3,2,1,0:T(8,128)} %a_ref.3), custom_call_target="tpu_custom_call" | custom-call | flops 14495514624 | bytes 75497472 | tf_op jit(solution)/shard_map/pallas_call | solution.py:43
  76.1 0.0 reduce-scatter.3.cloned.1.call-update
  76.1 0.0 all-gather.6.cloned.1.call-start
  76.1 40.5 %reduce-scatter.3.cloned.1.call-done = f32[768,128]{1,0:T(8,128)} async-done(((f32[6144,128]{1,0:T(8,128)}), f32[768,128]{1,0:T(8,128)}) %reduce-scatter.3.cloned.1.call-update) | async-done | bytes 393232 | tf_op jit(solution)/shard_map/reduce_scatter | solution.py:67
  116.6 0.0 all-gather.6.cloned.1.call-update
  116.6 0.0 reduce-scatter.5.cloned.1.call-start
  116.7 32.4 %all-gather.6.cloned.1.call-done.x_ref = f32[3072,128]{1,0:T(8,128)} async-done(((f32[768,128]{1,0:T(8,128)}), f32[3072,128]{1,0:T(8,128)}) %all-gather.6.cloned.1.call-update) | async-done | bytes 1572880 | tf_op jit(solution)/shard_map/all_gather | solution.py:65
  149.1 0.0 copy-start.1
  149.1 1.4 copy-done.1
  150.5 31.3 %shard_map.42 = f32[6144,128]{1,0:T(8,128)} custom-call(f32[3072,128]{1,0:T(8,128)S(1)} %copy-done.1, f32[4,1,768,6144]{3,2,1,0:T(8,128)} %a_ref.3), custom_call_target="tpu_custom_call" | custom-call | flops 14495514624 | bytes 75497472 | tf_op jit(solution)/shard_map/pallas_call | solution.py:43
  181.8 0.0 reduce-scatter.5.cloned.1.call-update
  181.8 40.5 %reduce-scatter.5.cloned.1.call-done = f32[768,128]{1,0:T(8,128)} async-done(((f32[6144,128]{1,0:T(8,128)}), f32[768,128]{1,0:T(8,128)}) %reduce-scatter.5.cloned.1.call-update) | async-done | bytes 393232 | tf_op jit(solution)/shard_map/reduce_scatter | solution.py:67
Async XLA Ops:
  7.2 36.2 %all-gather.4.cloned.1.call-start = ((), (), s32[]{:S(2)}) async-start(), calls=%async_computation.2 | async-start | bytes 1966080 | tf_op jit(solution)/shard_map/all_gather | solution.py:65
  7.9 108.7 %reduce-scatter.3.cloned.1.call-start = ((), (), s32[]{:S(2)}) async-start(), calls=%async_computation.3 | async-start | bytes 3538944 | tf_op jit(solution)/shard_map/reduce_scatter | solution.py:67
  43.4 1.4 copy-start
  76.1 73.0 %all-gather.6.cloned.1.call-start = ((), (), s32[]{:S(2)}) async-start(), calls=%async_computation.5 | async-start | bytes 1966080 | tf_op jit(solution)/shard_map/all_gather | solution.py:65
  116.6 105.7 %reduce-scatter.5.cloned.1.call-start = ((), (), s32[]{:S(2)}) async-start(), calls=%async_computation.4 | async-start | bytes 3538944 | tf_op jit(solution)/shard_map/reduce_scatter | solution.py:67
  149.1 1.4 copy-start.1
Sparse Core Ops, SparseCore 0:
  9.8 33.5 all-gather.3
  76.2 40.3 reduce-scatter.2
  119.0 30.0 all-gather.5
  181.9 40.3 reduce-scatter.4
where the time goes:
time: 230 us; the launch traced here: 229 us
  waiting for transfers between devices  150 us (65%)
  Pallas kernels  62.5 us (27%)
  between operations  13.8 us (6%)
  local copies, waits for them, and re-layouts  2.81 us (1%)
    reduce_scatter x2, waiting for transfers between devices, apply_once(): lax.psum_scatter(product(columns, inputs_flat), ('col', 'depth'), scatter...  81 us
    all_gather x2, waiting for transfers between devices, apply_once(): gathered = lax.all_gather(vector_part, 'row', axis=0, tiled=True)  67.9 us
    pallas_call x2, Pallas kernels, product(): pl.pallas_call(product_kernel, grid=(rows // tile,), out_shape=jax.ShapeD...  62.5 us
  transfers between devices with their start and end apart: 4, of which 4 were waited for; matrix products, arithmetic and copies ran while one was open for 0% of the time, Pallas kernels for 0%

commit v1 on v0

v1 whole, which is shorter than its diff:
```python
import functools
import math

import jax
import jax.numpy as jnp
from jax import lax
from jax.experimental import pallas as pl
from jax.experimental.pallas import tpu as pltpu
from jax.sharding import PartitionSpec as P

MESH = pl.DeviceIdType.MESH
LANES = 128
VMEM_BYTES = 67043328
VMEM_SPARE = 1 << 20
RING = 2
LAG = 3
PASSES = 2


def split(values):
    high = values.astype(jnp.bfloat16)
    low = (values - high.astype(jnp.float32)).astype(jnp.bfloat16)
    return high, low


class Plan:
    def __init__(self, mesh_shape, columns_shape, width):
        self.n_row = mesh_shape["row"]
        self.n_z = mesh_shape["col"]
        self.n_core = mesh_shape["depth"]
        assert self.n_core == 2
        side = math.isqrt(self.n_row)
        self.n_x = side if side * side == self.n_row else self.n_row
        self.n_y = self.n_row // self.n_x
        self.outer, _, self.piece, self.rows = columns_shape
        self.width = width
        self.fused = self.piece % LANES == 0 and self.n_z % 2 == 0
        self.chunk = LANES if self.fused else self.piece
        self.chunks = self.piece // self.chunk
        if self.fused:
            self.lanes = 4 * self.chunk
        else:
            self.lanes = math.gcd(self.rows, 4 * LANES)
        self.steps = self.rows // self.lanes
        self.pairs = self.n_z * self.chunks // 2
        self.k_depth = math.gcd(self.piece, 2 * LANES)
        self.core_base = 0 if self.fused else self.steps - 1
        self.base = self.core_base + 1
        last = 0
        for z in range(self.n_z):
            last = max(last, (self.n_z - 1 - z) * self.chunks - 1 + self.base + z * LAG)
            last = max(last, self.final_base(z, max) + self.chunks - 1)
        self.iterations = max(last + 1, self.steps, self.core_base + self.pairs)
        self.hops = (self.n_z - 1) * self.chunks
        step_bytes = 4 * self.outer * self.piece * self.lanes
        other = 4 * width * (
            self.rows
            + PASSES * self.n_z * self.chunks * self.chunk
            + 2 * PASSES * self.hops * self.chunk
            + PASSES * self.n_row * self.piece
            + (PASSES + 1) * self.piece
            + self.outer * self.piece
        )
        self.slots = min(self.steps, (VMEM_BYTES - VMEM_SPARE - other) // step_bytes)
        self.resident = self.steps if self.slots == self.steps else self.slots - RING
        self.ringed = self.steps - self.resident
        assert self.ringed == 0 or 0 <= 2 * self.resident <= self.steps

    def final_base(self, z, largest=jnp.maximum):
        right = (self.n_z - 1 - z) * self.chunks + z * LAG
        left = z * self.chunks + (self.n_z - 1 - z) * LAG
        if largest is max:
            if z == 0:
                return self.base + left
            if z == self.n_z - 1:
                return self.base + right
            return self.base + max(left, right)
        right = jnp.where(z > 0, right, 0)
        left = jnp.where(z < self.n_z - 1, left, 0)
        return self.base + largest(left, right)

    def scratch(self):
        f32 = jnp.float32
        chunk = (self.chunk, self.width)
        dma = pltpu.SemaphoreType.DMA
        pieces = self.n_z * self.chunks
        links = max(1, self.n_x + self.n_y - 2)
        relays = max(1, (self.n_x - 1) * (self.n_y - 1))
        parts = 4 if self.fused else 1
        return dict(
            a_buf=pltpu.VMEM((self.slots, self.outer, self.piece, self.lanes), f32),
            xt=pltpu.VMEM((self.outer, 2 * self.width, self.piece), jnp.bfloat16),
            acc=pltpu.VMEM((self.rows, self.width), f32),
            core_rx=pltpu.VMEM((PASSES, pieces) + chunk, f32),
            left_rx=pltpu.VMEM((PASSES, self.hops) + chunk, f32),
            right_rx=pltpu.VMEM((PASSES, self.hops) + chunk, f32),
            xg=pltpu.VMEM((PASSES, self.n_row, self.chunks) + chunk, f32),
            own=pltpu.VMEM((PASSES + 1, self.chunks) + chunk, f32),
            a_sem=dma((self.slots, parts)),
            io_sem=dma((3,)),
            ag_send=dma((PASSES, self.chunks, links)),
            ag_recv=dma((PASSES, self.n_row, self.chunks)),
            relay_send=dma((PASSES, self.chunks, relays)),
            core_send=dma((pieces,)),
            core_recv=dma((PASSES, pieces)),
            z_send=dma((pieces,)),
            left_recv=dma((PASSES, self.hops)),
            right_recv=dma((PASSES, self.hops)),
        )


def chain_kernel(
    plan, columns, source, first, second, *, a_buf, xt, acc, core_rx, left_rx, right_rx, xg, own,
    a_sem, io_sem, ag_send, ag_recv, relay_send, core_send, core_recv, z_send, left_recv, right_recv,
):
    n_z, n_x, n_y = plan.n_z, plan.n_x, plan.n_y
    chunk, chunks, width, piece = plan.chunk, plan.chunks, plan.width, plan.piece
    row, z, core = lax.axis_index("row"), lax.axis_index("col"), lax.axis_index("depth")
    x, y = lax.rem(row, n_x), lax.div(row, n_x)

    x_rows = [y * n_x + lax.rem(x + i, n_x) for i in range(1, n_x)]
    y_rows = [lax.rem(y + i, n_y) * n_x + x for i in range(1, n_y)]
    diagonal = [
        lax.rem(y + i, n_y) * n_x + lax.rem(x + k, n_x) for i in range(1, n_y) for k in range(1, n_x)
    ]
    left, right = (row, z - 1, core), (row, z + 1, core)
    partner = (row, z, 1 - core)

    def piece_chunks(pair):
        at, j = lax.div(pair, chunks), lax.rem(pair, chunks)
        return (n_z - 1 - at, j), (at, j)

    def row_start(at, on_core, j):
        return pl.multiple_of((at * 2 + on_core) * piece + j * chunk, 8 if not plan.fused else LANES)

    def loads(k, slot):
        if not plan.fused:
            lanes = pl.ds(pl.multiple_of(k * plan.lanes, LANES), plan.lanes)
            return [pltpu.make_async_copy(columns.at[:, 0, :, lanes], a_buf.at[slot], a_sem.at[slot, 0])]
        result = []
        for at, j in piece_chunks(k):
            for on_core in range(2):
                i = len(result)
                result.append(
                    pltpu.make_async_copy(
                        columns.at[:, 0, :, pl.ds(row_start(at, on_core, j), chunk)],
                        a_buf.at[slot, :, :, i * chunk:(i + 1) * chunk],
                        a_sem.at[slot, i],
                    )
                )
        return result

    def load(k, slot):
        for copy in loads(k, slot):
            copy.start()

    def ring_step(i):
        i = lax.rem(i, plan.ringed)
        return jnp.where(i <= plan.resident, 2 * i, plan.resident + i)

    def ring_slot(i):
        return plan.resident + lax.rem(i, RING)

    own_in = pltpu.make_async_copy(source, own.at[0], io_sem.at[0])
    own_in.start()
    if plan.ringed == 0:
        for k in range(plan.steps):
            load(k, k)
    else:
        for k in range(max(2 * plan.resident, 2 * RING)):
            if k % 2 == 1 and k < 2 * plan.resident:
                load(k, k // 2)
            if k % 2 == 0 and k < 2 * RING:
                load(ring_step(k // 2), ring_slot(k // 2))

    barrier = pltpu.get_barrier_semaphore()
    for other in x_rows + y_rows:
        pl.semaphore_signal(barrier, inc=1, device_id=(other, z, core), device_id_type=MESH)
    pl.semaphore_signal(barrier, inc=1, device_id=partner, device_id_type=MESH)

    @pl.when(z > 0)
    def _():
        pl.semaphore_signal(barrier, inc=1, device_id=left, device_id_type=MESH)

    @pl.when(z < n_z - 1)
    def _():
        pl.semaphore_signal(barrier, inc=1, device_id=right, device_id_type=MESH)

    beside = jnp.where(z > 0, 1, 0) + jnp.where(z < n_z - 1, 1, 0)
    pl.semaphore_wait(barrier, n_x + n_y - 1 + beside)

    own_in.wait()

    def spread(p, j, i, other):
        return pltpu.make_async_remote_copy(
            src_ref=own.at[p, j], dst_ref=xg.at[p, row, j],
            send_sem=ag_send.at[p, j, i], recv_sem=ag_recv.at[p, row, j],
            device_id=(other, z, core), device_id_type=MESH,
        )

    def relay(p, j, i, origin, other):
        return pltpu.make_async_remote_copy(
            src_ref=xg.at[p, origin, j], dst_ref=xg.at[p, origin, j],
            send_sem=relay_send.at[p, j, i], recv_sem=ag_recv.at[p, origin, j],
            device_id=(other, z, core), device_id_type=MESH,
        )

    def spread_all(p, j):
        for i, other in enumerate(x_rows + y_rows):
            spread(p, j, i, other).start()

    def place(origin, j, ref):
        high, low = split(ref[...].T)
        xt[origin, :width, j * chunk:(j + 1) * chunk] = high
        xt[origin, width:, j * chunk:(j + 1) * chunk] = low

    def gather(p):
        for j in range(chunks):
            place(row, j, own.at[p, j])
            near, far = (x_rows, y_rows) if j % 2 == 0 else (y_rows, x_rows)
            for i, origin in enumerate(near):
                relay(p, j, 0, origin, row).wait_recv()
                for k, other in enumerate(far):
                    relay(p, j, i * len(far) + k, origin, other).start()
                place(origin, j, xg.at[p, origin, j])
            for origin in far:
                relay(p, j, 0, origin, row).wait_recv()
                place(origin, j, xg.at[p, origin, j])
        for j in range(chunks):
            for origin in diagonal:
                relay(p, j, 0, origin, row).wait_recv()
                place(origin, j, xg.at[p, origin, j])

    def to_core(p, at, j):
        return pltpu.make_async_remote_copy(
            src_ref=acc.at[pl.ds(row_start(at, 1 - core, j), chunk), :],
            dst_ref=core_rx.at[p, at * chunks + j],
            send_sem=core_send.at[at * chunks + j], recv_sem=core_recv.at[p, at * chunks + j],
            device_id=partner, device_id_type=MESH,
        )

    def to_right(p, at, j):
        q = (n_z - 1 - at) * chunks + j
        return pltpu.make_async_remote_copy(
            src_ref=acc.at[pl.ds(row_start(at, core, j), chunk), :],
            dst_ref=left_rx.at[p, q],
            send_sem=z_send.at[at * chunks + j], recv_sem=left_recv.at[p, q],
            device_id=right, device_id_type=MESH,
        )

    def to_left(p, at, j):
        q = at * chunks + j
        return pltpu.make_async_remote_copy(
            src_ref=acc.at[pl.ds(row_start(at, core, j), chunk), :],
            dst_ref=right_rx.at[p, q],
            send_sem=z_send.at[at * chunks + j], recv_sem=right_recv.at[p, q],
            device_id=left, device_id_type=MESH,
        )

    def sent(p, at, j):
        to_core(p, at, j).wait_send()

        @pl.when(at > z)
        def _():
            to_right(p, at, j).wait_send()

        @pl.when(at < z)
        def _():
            to_left(p, at, j).wait_send()

    def multiply(p, k):
        if plan.ringed == 0:
            held, slot = True, k
        else:
            held = jnp.logical_and(lax.rem(k, 2) == 1, k < 2 * plan.resident)
            ring_at = p * plan.ringed + jnp.where(k < 2 * plan.resident, lax.div(k, 2), k - plan.resident)
            slot = jnp.where(held, lax.div(k, 2), ring_slot(ring_at))

        @pl.when(jnp.logical_or(p == 0, jnp.logical_not(held)))
        def _():
            for copy in loads(k, slot):
                copy.wait()

        main = rest = None
        for a in range(plan.outer):
            for at in range(0, piece, plan.k_depth):
                span = slice(at, at + plan.k_depth)
                high, low = split(a_buf[slot, a, span, :])
                both = jnp.dot(xt[a, :, span], high, preferred_element_type=jnp.float32)
                side = jnp.dot(xt[a, :width, span], low, preferred_element_type=jnp.float32)
                main = both if main is None else main + both
                rest = side if rest is None else rest + side
        total = (main[:width] + (main[width:] + rest)).T
        if plan.fused:
            i = 0
            for at, j in piece_chunks(k):
                for on_core in range(2):
                    acc[pl.ds(row_start(at, on_core, j), chunk), :] = total[i * chunk:(i + 1) * chunk]
                    i += 1
        else:
            acc[pl.ds(pl.multiple_of(k * plan.lanes, LANES), plan.lanes), :] = total

        if plan.ringed > 0:
            follow = ring_at + RING

            @pl.when(jnp.logical_and(jnp.logical_not(held), follow < PASSES * plan.ringed))
            def _():
                load(ring_step(follow), ring_slot(follow))

    def own_sum(p, at, j):
        to_core(p, at, j).wait_recv()
        mine = pl.ds(row_start(at, core, j), chunk)
        acc[mine, :] = acc[mine, :] + core_rx[p, at * chunks + j]
        return mine

    def iteration(k, p):
        @pl.when(k < plan.steps)
        def _():
            @pl.when(p > 0)
            def _():
                if plan.fused:
                    for at, j in piece_chunks(k):
                        sent(p, at, j)
                else:
                    @pl.when(k == 0)
                    def _():
                        sent_all(p)
            multiply(p, k)

        pair = k - plan.core_base

        @pl.when(jnp.logical_and(pair >= 0, pair < plan.pairs))
        def _():
            for at, j in piece_chunks(pair):
                to_core(p, at, j).start()

        q = k - plan.base - z * LAG

        @pl.when(jnp.logical_and(q >= 0, q < (n_z - 1 - z) * chunks))
        def _():
            at, j = n_z - 1 - lax.div(q, chunks), lax.rem(q, chunks)
            mine = own_sum(p, at, j)

            @pl.when(z > 0)
            def _():
                to_right(p, at, j).wait_recv()
                acc[mine, :] = acc[mine, :] + left_rx[p, q]

            to_right(p, at, j).start()

        s = k - plan.base - (n_z - 1 - z) * LAG

        @pl.when(jnp.logical_and(s >= 0, s < z * chunks))
        def _():
            at, j = lax.div(s, chunks), lax.rem(s, chunks)
            mine = own_sum(p, at, j)

            @pl.when(z < n_z - 1)
            def _():
                to_left(p, at, j).wait_recv()
                acc[mine, :] = acc[mine, :] + right_rx[p, s]

            to_left(p, at, j).start()

        f = k - plan.final_base(z)

        @pl.when(jnp.logical_and(f >= 0, f < chunks))
        def _():
            mine = own_sum(p, z, f)

            @pl.when(z > 0)
            def _():
                to_right(p, z, f).wait_recv()
                acc[mine, :] = acc[mine, :] + left_rx[p, (n_z - 1 - z) * chunks + f]

            @pl.when(z < n_z - 1)
            def _():
                to_left(p, z, f).wait_recv()
                acc[mine, :] = acc[mine, :] + right_rx[p, z * chunks + f]

            own[p + 1, f] = acc[mine, :]

            @pl.when(p + 1 < PASSES)
            def _():
                spread_all(p + 1, f)

        return p

    def sent_all(p):
        def one(i, carry):
            sent(p, lax.div(i, chunks), lax.rem(i, chunks))
            return carry

        lax.fori_loop(0, n_z * chunks, one, 0)

    out_first = pltpu.make_async_copy(own.at[1], first, io_sem.at[1])
    out_second = pltpu.make_async_copy(own.at[2], second, io_sem.at[2])

    for j in range(chunks):
        spread_all(0, j)

    def one_pass(p, carry):
        gather(p)
        lax.fori_loop(0, plan.iterations, iteration, p)

        @pl.when(p == 0)
        def _():
            out_first.start()

        return carry

    lax.fori_loop(0, PASSES, one_pass, 0)
    out_second.start()
    sent_all(PASSES - 1)
    for p in range(PASSES):
        for j in range(chunks):
            for i, other in enumerate(x_rows + y_rows):
                spread(p, j, i, other).wait_send()
            for i in range((n_x - 1) * (n_y - 1)):
                relay(p, j, i, row, row).wait_send()
    out_first.wait()
    out_second.wait()


def solution(mesh):
    def body(matrix_columns, sources):
        plan = Plan(dict(mesh.shape), matrix_columns.shape, sources.shape[-1])
        blocked = (plan.chunks, plan.chunk, plan.width)
        image = jax.ShapeDtypeStruct(blocked, jnp.float32)
        anywhere = pl.BlockSpec(memory_space=pl.ANY)
        scratch = plan.scratch()
        products = PASSES * plan.rows * plan.outer * plan.piece
        first, second = pl.pallas_call(
            functools.partial(chain_kernel, plan),
            out_shape=(image, image),
            in_specs=[anywhere, anywhere],
            out_specs=(anywhere, anywhere),
            scratch_shapes=scratch,
            compiler_params=pltpu.CompilerParams(
                collective_id=0, has_side_effects=True, vmem_limit_bytes=VMEM_BYTES
            ),
            cost_estimate=pl.CostEstimate(
                flops=6 * products * plan.width, bytes_accessed=4 * products, transcendentals=0
            ),
        )(matrix_columns, sources.reshape(blocked))
        return first.reshape(sources.shape), second.reshape(sources.shape)

    in_specs = (P(None, ("col", "depth"), None, "row"), P("row", ("col", "depth"), None, None))
    out_specs = (P("row", ("col", "depth"), None, None), P("row", ("col", "depth"), None, None))
    return jax.shard_map(body, mesh=mesh, in_specs=in_specs, out_specs=out_specs, check_vma=False)
```

time: 230 us -> 108 us (0.47)
  the two profiles are of different devices: /device:TPU:0 before, /device:TPU:10 now
where the time goes in v1:
time: 108 us; the launch traced here: 107 us
  Pallas kernels  103 us (95%)
  local copies, waits for them, and re-layouts  3.53 us (3%)
    pallas_call x1, Pallas kernels, body(): pl.pallas_call(functools.partial(chain_kernel, plan), out_shape=(image, i...  103 us
    unnamed x2, local copies, waits for them, and re-layouts  3.53 us

profile of v1, /device:TPU:10, one launch (start us, length us, event | category | flops | bytes accessed | tf_op | source)
XLA Modules:
  0.0 106.8 jit_solution(8903175795375790044)
XLA Ops:
  0.6 102.6 %shard_map.41 = (f32[6,128,128]{2,1,0:T(8,128)}, f32[6,128,128]{2,1,0:T(8,128)}) custom-call(f32[4,1,768,6144]{3,2,1,0:T(8,128)} %columns.1, f32[6,128,128]{2,1,0:T(8,128)} %bitcast.5), custom_call_target="tpu_custom_call" | custom-call | flops 28991029248 | bytes 150994944 | tf_op jit(solution)/shard_map/pallas_call | solution.py:433
  103.3 1.8 %copy.6 = f32[1,1,768,128]{3,2,1,0:T(8,128)} copy(f32[1,1,768,128]{3,2,1,0:T(8,128)} %bitcast.4) | data formatting | bytes 786432
  105.0 1.8 %copy.7 = f32[1,1,768,128]{3,2,1,0:T(8,128)} copy(f32[1,1,768,128]{3,2,1,0:T(8,128)} %bitcast.3) | data formatting | bytes 786432

commit v2 on v1

v2 whole, which is shorter than its diff:
```python
import functools
import math

import jax
import jax.numpy as jnp
from jax import lax
from jax.experimental import pallas as pl
from jax.experimental.pallas import tpu as pltpu
from jax.sharding import PartitionSpec as P

MESH = pl.DeviceIdType.MESH
LANES = 128
VMEM_BYTES = 67043328
VMEM_SPARE = 256 << 10
RING = 2
LAG = 3
RELAY = 2
PASSES = 2


def split(values):
    high = values.astype(jnp.bfloat16)
    low = (values - high.astype(jnp.float32)).astype(jnp.bfloat16)
    return high, low


class Plan:
    def __init__(self, mesh_shape, columns_shape, width):
        self.n_row = mesh_shape["row"]
        self.n_z = mesh_shape["col"]
        assert mesh_shape["depth"] == 2
        side = math.isqrt(self.n_row)
        self.n_x = side if side * side == self.n_row else self.n_row
        self.n_y = self.n_row // self.n_x
        self.outer, _, self.piece, self.rows = columns_shape
        self.width = width
        self.fused = self.piece % LANES == 0 and self.n_z % 2 == 0 and self.n_z >= 4
        self.chunk = LANES if self.fused else self.piece
        self.chunks = self.piece // self.chunk
        self.per_step = 4 if self.fused else math.lcm(self.piece, LANES) // self.piece
        self.lanes = self.per_step * self.chunk
        self.steps = self.rows // self.lanes
        self.ids = self.n_z * self.chunks
        self.k_depth = math.gcd(self.piece, 2 * LANES)
        self.base = 1 if self.fused else self.steps
        finals = max(self.final_start(z) for z in range(self.n_z)) + self.chunks
        self.period = max(self.steps, finals + RELAY)
        self.arrivals = (self.n_z + 1) * self.chunks
        step_bytes = 4 * self.outer * self.piece * self.lanes
        lanes_padded = -(-self.chunk // LANES) * LANES
        other = 4 * self.width * lanes_padded * (
            4 * self.ids
            + PASSES * self.ids
            + PASSES * self.arrivals
            + PASSES * self.n_row * self.chunks
            + (PASSES + 1) * self.chunks
        ) + 4 * self.width * self.outer * self.piece + 8 * self.piece * width
        self.slots = min(self.steps, (VMEM_BYTES - VMEM_SPARE - other) // step_bytes)
        self.resident = self.steps if self.slots == self.steps else self.slots - RING
        self.ringed = self.steps - self.resident
        assert self.ringed == 0 or 0 <= 2 * self.resident <= self.steps

    def final_start(self, z):
        n_z, n = self.n_z, self.chunks
        from_left = (n_z - 1 - z) * n + (0 if self.fused and z == 1 else z * LAG)
        from_right = z * n + (0 if self.fused and z == n_z - 2 else (n_z - 1 - z) * LAG)
        if z == 0:
            from_left = 0
        if z == n_z - 1:
            from_right = 0
        return self.base + max(from_left, from_right)

    def scratch(self):
        f32 = jnp.float32
        chunk = (self.width, self.chunk)
        dma = pltpu.SemaphoreType.DMA
        links = max(1, self.n_x + self.n_y - 2)
        relays = max(1, (self.n_x - 1) * (self.n_y - 1))
        parts = 4 if self.fused else 1
        return dict(
            a_buf=pltpu.VMEM((self.slots, self.outer, self.piece, self.lanes), f32),
            xt=pltpu.VMEM((self.outer, 2 * self.width, self.piece), jnp.bfloat16),
            acc=pltpu.VMEM((PASSES, 2 * self.ids) + chunk, f32),
            core_rx=pltpu.VMEM((PASSES, self.ids) + chunk, f32),
            z_rx=pltpu.VMEM((PASSES, self.arrivals) + chunk, f32),
            xg=pltpu.VMEM((PASSES, self.n_row, self.chunks) + chunk, f32),
            own=pltpu.VMEM((PASSES + 1, self.chunks) + chunk, f32),
            edge=pltpu.VMEM((2, self.chunks, self.chunk, self.width), f32),
            a_sem=dma((self.slots, parts)),
            in_sem=dma(()),
            out_sem=dma((2, self.chunks)),
            ag_send=dma((PASSES, self.chunks, links)),
            ag_recv=dma((PASSES, self.n_row, self.chunks)),
            relay_send=dma((PASSES, self.chunks, relays)),
            core_send=dma((PASSES, self.ids)),
            core_recv=dma((PASSES, self.ids)),
            z_send=dma((PASSES, self.ids)),
            z_recv=dma((PASSES, self.arrivals)),
        )


def chain_kernel(
    plan, columns, source, first, second, *, a_buf, xt, acc, core_rx, z_rx, xg, own, edge,
    a_sem, in_sem, out_sem, ag_send, ag_recv, relay_send, core_send, core_recv, z_send, z_recv,
):
    n_z, n_x, n_y = plan.n_z, plan.n_x, plan.n_y
    chunk, chunks, width, piece = plan.chunk, plan.chunks, plan.width, plan.piece
    steps = plan.steps
    row, z, core = lax.axis_index("row"), lax.axis_index("col"), lax.axis_index("depth")
    x, y = lax.rem(row, n_x), lax.div(row, n_x)
    at_left, at_right = z == 0, z == n_z - 1

    x_rows = [y * n_x + lax.rem(x + i, n_x) for i in range(1, n_x)]
    y_rows = [lax.rem(y + i, n_y) * n_x + x for i in range(1, n_y)]
    diagonal = [
        lax.rem(y + i, n_y) * n_x + lax.rem(x + k, n_x) for i in range(1, n_y) for k in range(1, n_x)
    ]
    left, right = (row, z - 1, core), (row, z + 1, core)
    partner = (row, z, 1 - core)

    def piece_of(at):
        return sum(jnp.where(at >= n * chunks, 1, 0) for n in range(1, n_z))

    def rightward(q):
        return q + (n_z - 1 - 2 * piece_of(q)) * chunks

    def place_of(at, on_core):
        return at + (piece_of(at) + on_core) * chunks

    def step_ids(k):
        one = jnp.where(at_left, rightward(2 * k), jnp.where(at_right, 2 * k, rightward(k)))
        two = jnp.where(at_left, rightward(2 * k + 1), jnp.where(at_right, 2 * k + 1, k))
        return one, two

    def loads(k, slot):
        if not plan.fused:
            lanes = pl.ds(pl.multiple_of(k * plan.lanes, LANES), plan.lanes)
            return [pltpu.make_async_copy(columns.at[:, 0, :, lanes], a_buf.at[slot], a_sem.at[slot, 0])]
        result = []
        for at in step_ids(k):
            for on_core in range(2):
                i = len(result)
                lanes = pl.ds(pl.multiple_of(place_of(at, on_core) * chunk, LANES), chunk)
                result.append(
                    pltpu.make_async_copy(
                        columns.at[:, 0, :, lanes],
                        a_buf.at[slot, :, :, i * chunk:(i + 1) * chunk],
                        a_sem.at[slot, i],
                    )
                )
        return result

    def load(k, slot):
        for copy in loads(k, slot):
            copy.start(priority=1)

    def ring_step(i):
        i = jnp.where(i >= plan.ringed, i - plan.ringed, i)
        return jnp.where(i <= plan.resident, 2 * i, plan.resident + i)

    def ring_slot(i):
        return plan.resident + lax.rem(i, RING)

    source_in = pltpu.make_async_copy(source, edge.at[0], in_sem)
    source_in.start()
    if plan.ringed == 0:
        for k in range(steps):
            load(k, k)
    else:
        for k in range(max(2 * plan.resident, 2 * RING)):
            if k % 2 == 1 and k < 2 * plan.resident:
                load(k, k // 2)
            if k % 2 == 0 and k < 2 * RING:
                load(ring_step(k // 2), ring_slot(k // 2))

    barrier = pltpu.get_barrier_semaphore()
    for other in x_rows + y_rows:
        pl.semaphore_signal(barrier, inc=1, device_id=(other, z, core), device_id_type=MESH)
    pl.semaphore_signal(barrier, inc=1, device_id=partner, device_id_type=MESH)

    @pl.when(jnp.logical_not(at_left))
    def _():
        pl.semaphore_signal(barrier, inc=1, device_id=left, device_id_type=MESH)

    @pl.when(jnp.logical_not(at_right))
    def _():
        pl.semaphore_signal(barrier, inc=1, device_id=right, device_id_type=MESH)

    beside = jnp.where(at_left, 0, 1) + jnp.where(at_right, 0, 1)

    source_in.wait()
    for j in range(chunks):
        own[0, j] = edge[0, j].T

    pl.semaphore_wait(barrier, n_x + n_y - 1 + beside)

    def spread(p, j, i, other):
        return pltpu.make_async_remote_copy(
            src_ref=own.at[p, j], dst_ref=xg.at[p, row, j],
            send_sem=ag_send.at[p, j, i], recv_sem=ag_recv.at[p, row, j],
            device_id=(other, z, core), device_id_type=MESH,
        )

    def relay(p, j, i, origin, other):
        return pltpu.make_async_remote_copy(
            src_ref=xg.at[p, origin, j], dst_ref=xg.at[p, origin, j],
            send_sem=relay_send.at[p, j, i], recv_sem=ag_recv.at[p, origin, j],
            device_id=(other, z, core), device_id_type=MESH,
        )

    def spread_all(p, j):
        for i, other in enumerate(x_rows + y_rows):
            spread(p, j, i, other).start()

    def pass_on(p, j, near, far):
        for i, origin in enumerate(near):
            relay(p, j, 0, origin, row).wait_recv()
            for k, other in enumerate(far):
                relay(p, j, i * len(far) + k, origin, other).start()

    def place(origin, j, ref):
        high, low = split(ref[...])
        xt[origin, :width, j * chunk:(j + 1) * chunk] = high
        xt[origin, width:, j * chunk:(j + 1) * chunk] = low

    def sides(j):
        return (x_rows, y_rows) if j % 2 == 0 else (y_rows, x_rows)

    def gather(p):
        @pl.when(p == 0)
        def _():
            for j in range(chunks):
                pass_on(p, j, *sides(j))

        for j in range(chunks):
            near, far = sides(j)
            place(row, j, own.at[p, j])
            for origin in near:
                place(origin, j, xg.at[p, origin, j])
            for origin in far:
                relay(p, j, 0, origin, row).wait_recv()
                place(origin, j, xg.at[p, origin, j])
        for j in range(chunks):
            for origin in diagonal:
                relay(p, j, 0, origin, row).wait_recv()
                place(origin, j, xg.at[p, origin, j])

    def to_core(p, at):
        return pltpu.make_async_remote_copy(
            src_ref=acc.at[p, place_of(at, 1 - core)],
            dst_ref=core_rx.at[p, at],
            send_sem=core_send.at[p, at], recv_sem=core_recv.at[p, at],
            device_id=partner, device_id_type=MESH,
        )

    def along(p, at, slot, other):
        return pltpu.make_async_remote_copy(
            src_ref=acc.at[p, place_of(at, core)],
            dst_ref=z_rx.at[p, slot],
            send_sem=z_send.at[p, at], recv_sem=z_recv.at[p, slot],
            device_id=other, device_id_type=MESH,
        )

    def to_right(p, q):
        return along(p, rightward(q), q, right)

    def to_left(p, q):
        return along(p, q, plan.arrivals - 1 - q, left)

    def sent(p, at):
        to_core(p, at).wait_send()

        @pl.when(piece_of(at) != z)
        def _():
            along(p, at, 0, right).wait_send()

    def sent_all(p):
        def one(at, carry):
            sent(p, at)
            return carry

        lax.fori_loop(0, plan.ids, one, 0)

    def multiply(p, k):
        if plan.ringed == 0:
            held, slot = True, k
        else:
            held = jnp.logical_and(lax.rem(k, 2) == 1, k < 2 * plan.resident)
            ring_at = p * plan.ringed + jnp.where(k < 2 * plan.resident, lax.div(k, 2), k - plan.resident)
            slot = jnp.where(held, lax.div(k, 2), ring_slot(ring_at))

        @pl.when(jnp.logical_or(p == 0, jnp.logical_not(held)))
        def _():
            for copy in loads(k, slot):
                copy.wait()

        main = rest = None
        for a in range(plan.outer):
            for at in range(0, piece, plan.k_depth):
                span = slice(at, at + plan.k_depth)
                high, low = split(a_buf[slot, a, span, :])
                both = jnp.dot(xt[a, :, span], high, preferred_element_type=jnp.float32)
                side = jnp.dot(xt[a, :width, span], low, preferred_element_type=jnp.float32)
                main = both if main is None else main + both
                rest = side if rest is None else rest + side
        total = main[:width] + (main[width:] + rest)
        if plan.fused:
            at = [place_of(at, on_core) for at in step_ids(k) for on_core in range(2)]
        else:
            at = [k * plan.per_step + i for i in range(plan.per_step)]
        for i, where in enumerate(at):
            acc[p, where] = total[:, i * chunk:(i + 1) * chunk]

        if plan.ringed > 0:
            follow = ring_at + RING

            @pl.when(jnp.logical_and(jnp.logical_not(held), follow < PASSES * plan.ringed))
            def _():
                load(ring_step(follow), ring_slot(follow))

    def own_sum(p, at):
        to_core(p, at).wait_recv()
        mine = place_of(at, core)
        acc[p, mine] = acc[p, mine] + core_rx[p, at]
        return mine

    def add_from_left(p, q, mine):
        to_right(p, q).wait_recv()
        acc[p, mine] = acc[p, mine] + z_rx[p, q]

    def add_from_right(p, q, mine):
        to_left(p, q).wait_recv()
        acc[p, mine] = acc[p, mine] + z_rx[p, plan.arrivals - 1 - q]

    def finish(p, f):
        mine = own_sum(p, z * chunks + f)

        @pl.when(jnp.logical_not(at_left))
        def _():
            add_from_left(p, (n_z - 1 - z) * chunks + f, mine)

        @pl.when(jnp.logical_not(at_right))
        def _():
            add_from_right(p, z * chunks + f, mine)

        image = acc[p, mine]
        own[p + 1, f] = image
        edge[p, f] = image.T

        @pl.when(p == 0)
        def _():
            spread_all(1, f)
            pltpu.make_async_copy(edge.at[0, f], first.at[f], out_sem.at[0, f]).start()

        @pl.when(p == 1)
        def _():
            pltpu.make_async_copy(edge.at[1, f], second.at[f], out_sem.at[1, f]).start()

    first_final = sum(jnp.where(z == at, plan.final_start(at), 0) for at in range(n_z))

    def iteration(i, p):
        k = i

        @pl.when(k < steps)
        def _():
            multiply(p, k)

            if plan.fused:
                for at in step_ids(k):
                    to_core(p, at).start()
            else:
                @pl.when(k == steps - 1)
                def _():
                    def one(at, inner):
                        to_core(p, at).start()
                        return inner

                    lax.fori_loop(0, plan.ids, one, 0)

        w = i - plan.base - z * LAG
        for u in range(2 if plan.fused else 1):
            q = jnp.where(at_left, 2 * w + u, w) if plan.fused else w
            also = jnp.logical_or(u == 0, at_left)
            inside = jnp.logical_and(w >= 0, q < (n_z - 1 - z) * chunks)

            @pl.when(jnp.logical_and(also, inside))
            def _(q=q):
                mine = own_sum(p, rightward(q))

                @pl.when(jnp.logical_not(at_left))
                def _():
                    add_from_left(p, q, mine)

                to_right(p, q).start()

        w = i - plan.base - (n_z - 1 - z) * LAG
        for u in range(2 if plan.fused else 1):
            q = jnp.where(at_right, 2 * w + u, w) if plan.fused else w
            also = jnp.logical_or(u == 0, at_right)
            inside = jnp.logical_and(w >= 0, q < z * chunks)

            @pl.when(jnp.logical_and(also, inside))
            def _(q=q):
                mine = own_sum(p, q)

                @pl.when(jnp.logical_not(at_right))
                def _():
                    add_from_right(p, q, mine)

                to_left(p, q).start()

        f = i - first_final

        @pl.when(jnp.logical_and(f >= 0, f < chunks))
        def _():
            finish(p, f)

        j = f - RELAY
        due = jnp.logical_and(p + 1 < PASSES, jnp.logical_and(j >= 0, j < chunks))
        for parity in range(2):
            @pl.when(jnp.logical_and(due, lax.rem(j, 2) == parity))
            def _(parity=parity):
                pass_on(p + 1, j, *sides(parity))

        return p

    for j in range(chunks):
        spread_all(0, j)

    def one_pass(p, carry):
        gather(p)
        lax.fori_loop(0, plan.period, iteration, p)
        return carry

    lax.fori_loop(0, PASSES, one_pass, 0)

    sent_all(0)
    sent_all(1)
    for p in range(PASSES):
        for j in range(chunks):
            for i, other in enumerate(x_rows + y_rows):
                spread(p, j, i, other).wait_send()
            for i in range((n_x - 1) * (n_y - 1)):
                relay(p, j, i, row, row).wait_send()
    for j in range(chunks):
        pltpu.make_async_copy(edge.at[0, j], first.at[j], out_sem.at[0, j]).wait()
        pltpu.make_async_copy(edge.at[1, j], second.at[j], out_sem.at[1, j]).wait()


def solution(mesh):
    def body(matrix_columns, sources):
        plan = Plan(dict(mesh.shape), matrix_columns.shape, sources.shape[-1])
        blocked = (plan.chunks, plan.chunk, plan.width)
        image = jax.ShapeDtypeStruct(blocked, jnp.float32)
        anywhere = pl.BlockSpec(memory_space=pl.ANY)
        products = 2 * plan.rows * plan.outer * plan.piece
        first, second = pl.pallas_call(
            functools.partial(chain_kernel, plan),
            out_shape=(image, image),
            in_specs=[anywhere, anywhere],
            out_specs=(anywhere, anywhere),
            scratch_shapes=plan.scratch(),
            compiler_params=pltpu.CompilerParams(
                collective_id=0, has_side_effects=True, vmem_limit_bytes=VMEM_BYTES
            ),
            cost_estimate=pl.CostEstimate(
                flops=6 * products * plan.width, bytes_accessed=4 * products, transcendentals=0
            ),
        )(matrix_columns, sources.reshape(blocked))
        return first.reshape(sources.shape), second.reshape(sources.shape)

    in_specs = (P(None, ("col", "depth"), None, "row"), P("row", ("col", "depth"), None, None))
    out_specs = (P("row", ("col", "depth"), None, None), P("row", ("col", "depth"), None, None))
    return jax.shard_map(body, mesh=mesh, in_specs=in_specs, out_specs=out_specs, check_vma=False)
```

time: 108 us -> 92.5 us (0.86)
  Pallas kernels: 103 us -> 88.1 us
    pallas_call x1, Pallas kernels: 103 us -> 88.1 us  [body(): pl.pallas_call(functools.partial(chain_kernel, plan), out_shape=(image, i...]
where the time goes in v2:
time: 92.5 us; the launch traced here: 92.3 us
  Pallas kernels  88.1 us (95%)
  local copies, waits for them, and re-layouts  3.53 us (4%)
    pallas_call x1, Pallas kernels, body(): pl.pallas_call(functools.partial(chain_kernel, plan), out_shape=(image, i...  88.1 us
    unnamed x2, local copies, waits for them, and re-layouts  3.53 us

profile of v2, /device:TPU:10, one launch (start us, length us, event | category | flops | bytes accessed | tf_op | source)
XLA Modules:
  0.0 92.3 jit_solution(12719398295705991943)
XLA Ops:
  0.6 88.1 %shard_map.41 = (f32[6,128,128]{2,1,0:T(8,128)}, f32[6,128,128]{2,1,0:T(8,128)}) custom-call(f32[4,1,768,6144]{3,2,1,0:T(8,128)} %columns.1, f32[6,128,128]{2,1,0:T(8,128)} %bitcast.5), custom_call_target="tpu_custom_call" | custom-call | flops 28991029248 | bytes 150994944 | tf_op jit(solution)/shard_map/pallas_call | solution.py:457
  88.7 1.8 %copy.6 = f32[1,1,768,128]{3,2,1,0:T(8,128)} copy(f32[1,1,768,128]{3,2,1,0:T(8,128)} %bitcast.4) | data formatting | bytes 786432
  90.5 1.8 %copy.7 = f32[1,1,768,128]{3,2,1,0:T(8,128)} copy(f32[1,1,768,128]{3,2,1,0:T(8,128)} %bitcast.3) | data formatting | bytes 786432

commit v3 on v2

--- a/solution.py
+++ b/solution.py
@@ -377,7 +377,7 @@
 
                     lax.fori_loop(0, plan.ids, one, 0)
 
-        w = i - plan.base - z * LAG
+        w = i - plan.base - z * LAG + jnp.where(jnp.logical_and(p > 0, z > 0), LAG - 1, 0)
         for u in range(2 if plan.fused else 1):
             q = jnp.where(at_left, 2 * w + u, w) if plan.fused else w
             also = jnp.logical_or(u == 0, at_left)
@@ -393,7 +393,7 @@
 
                 to_right(p, q).start()
 
-        w = i - plan.base - (n_z - 1 - z) * LAG
+        w = i - plan.base - (n_z - 1 - z) * LAG + jnp.where(jnp.logical_and(p > 0, z < n_z - 1), LAG - 1, 0)
         for u in range(2 if plan.fused else 1):
             q = jnp.where(at_right, 2 * w + u, w) if plan.fused else w
             also = jnp.logical_or(u == 0, at_right)
@@ -445,6 +445,11 @@
     for j in range(chunks):
         pltpu.make_async_copy(edge.at[0, j], first.at[j], out_sem.at[0, j]).wait()
         pltpu.make_async_copy(edge.at[1, j], second.at[j], out_sem.at[1, j]).wait()
+
+
+def hand_over(first_in, second_in, first, second):
+    first[...] = first_in[...]
+    second[...] = second_in[...]
 
 
 def solution(mesh):
@@ -467,6 +472,12 @@
                 flops=6 * products * plan.width, bytes_accessed=4 * products, transcendentals=0
             ),
         )(matrix_columns, sources.reshape(blocked))
+        first, second = pl.pallas_call(
+            hand_over,
+            out_shape=(image, image),
+            in_specs=[pl.BlockSpec(memory_space=pltpu.VMEM)] * 2,
+            out_specs=(pl.BlockSpec(memory_space=pltpu.VMEM),) * 2,
+        )(first, second)
         return first.reshape(sources.shape), second.reshape(sources.shape)
 
     in_specs = (P(None, ("col", "depth"), None, "row"), P("row", ("col", "depth"), None, None))

time: 92.5 us -> 88.7 us (0.959)
  local copies, waits for them, and re-layouts: 3.53 us -> 0 us
    unnamed x2 -> x0, local copies, waits for them, and re-layouts: 3.53 us -> none
    pallas_call x1, Pallas kernels: 88.1 us -> 85.9 us  [body(): pl.pallas_call(functools.partial(chain_kernel, plan), out_shape=(image, i...]
    pallas_call x0 -> x1, Pallas kernels: none -> 2.02 us  [body(): pl.pallas_call(hand_over, out_shape=(image, image), in_specs=[pl.BlockSpe...]
where the time goes in v3:
time: 88.7 us; the launch traced here: 88.6 us
  Pallas kernels  87.9 us (99%)
    pallas_call x1, Pallas kernels, body(): pl.pallas_call(functools.partial(chain_kernel, plan), out_shape=(image, i...  85.9 us
    pallas_call x1, Pallas kernels, body(): pl.pallas_call(hand_over, out_shape=(image, image), in_specs=[pl.BlockSpe...  2.02 us

profile of v3, /device:TPU:10, one launch (start us, length us, event | category | flops | bytes accessed | tf_op | source)
XLA Modules:
  0.0 88.6 jit_solution(7929668239174609359)
XLA Ops:
  0.6 85.9 %shard_map.41 = (f32[6,128,128]{2,1,0:T(8,128)}, f32[6,128,128]{2,1,0:T(8,128)}) custom-call(f32[4,1,768,6144]{3,2,1,0:T(8,128)} %columns.1, f32[6,128,128]{2,1,0:T(8,128)} %bitcast.3), custom_call_target="tpu_custom_call" | custom-call | flops 28991029248 | bytes 150994944 | tf_op jit(solution)/shard_map/pallas_call | solution.py:462
  86.6 2.0 %shard_map.42 = (f32[6,128,128]{2,1,0:T(8,128)}, f32[6,128,128]{2,1,0:T(8,128)}) custom-call(f32[6,128,128]{2,1,0:T(8,128)} %get-tuple-element.6.first_in, f32[6,128,128]{2,1,0:T(8,128)} %get-tuple-element.7.second_in), custom_call_target="tpu_custom_call" | custom-call | tf_op jit(solution)/shard_map/pallas_call | solution.py:475
